TPU v7x, 32 devices: a whole 2x2x4 slice. The times are simulated.
32 devices in a mesh: row: 4 (over y, x), col: 8 (over z, core).
Axes of the slice: x: 2, y: 2, z: 4, core: 2. Of those that a mesh axis runs over, the one named last changes fastest.
Arguments:
- covariance: float32 [16384, 16384], P('row', 'col'), may hold values from -1 to 560
- seed_index: int32 [128], replicated, may hold values from 0 to 16383, as said below
Outputs:
- basis: float32 [16384, 384], P('row')
- projection: float32 [384, 256], replicated
- first_pass: float32 [384, 256], replicated
Inputs may be any that keep to these rules, and one draw needn't show every extreme that they name: `seed_index`: 128 distinct column indices.
All inputs are finite; a program needn't handle non-finite values.
Results may differ from a plain program's by a relative error of at most 0.00019.
Values sent between devices are 32-bit elements; how exact they have to be, the bound alone decides.
A program may use at most 128 MiB of HBM per device.

v0:
```python
import jax
import jax.numpy as jnp
from jax import lax
from jax.sharding import PartitionSpec as P

N = 16384
ITERS = 2


def product(left, right):
    return jnp.dot(left, right, precision=lax.Precision.HIGHEST, preferred_element_type=jnp.float32)


def finish_block(block, gram):
    lower = jnp.linalg.cholesky(gram)
    basis_block = jax.scipy.linalg.solve_triangular(lower, block.T, lower=True).T
    return (basis_block, lower.T)


def transpose_block(current, col_place, col_count):
    whole = lax.all_gather(current, "row", axis=0, tiled=True)
    vector = lax.dynamic_slice_in_dim(whole, col_place * col_count, col_count, 0)
    return vector


def local(covariance, seed_index):
    col_count = covariance.shape[1]
    width = seed_index.shape[0]
    col_place = lax.axis_index("col")
    offsets = seed_index - col_place * col_count
    inside = (offsets >= 0) & (offsets < col_count)
    picked = jnp.take(covariance, jnp.clip(offsets, 0, col_count - 1), axis=1)
    start = lax.psum(jnp.where(inside[None, :], picked, 0.0), "col")
    gram = lax.psum(product(start.T, start), "row")
    current, upper = finish_block(start, gram)
    full = current
    blocks = [current]
    projection = jnp.zeros(((ITERS + 1) * width, ITERS * width), jnp.float32)
    first_pass = jnp.zeros(((ITERS + 1) * width, ITERS * width), jnp.float32)
    for section in range(ITERS):
        vector = transpose_block(full, col_place, col_count)
        partial_value = product(covariance, vector)
        stacked = jnp.concatenate(blocks, axis=1)
        image = lax.psum(partial_value, "col")
        first = lax.psum(product(stacked.T, image), "row")
        once = image - product(stacked, first)
        second, raw_gram = lax.psum((product(stacked.T, once), product(once.T, once)), "row")
        twice = once - product(stacked, second)
        gram = raw_gram - product(second.T, second)
        current, upper = finish_block(twice, gram)
        projection = projection.at[
            : (section + 1) * width, section * width : (section + 1) * width
        ].set(first + second)
        projection = projection.at[
            (section + 1) * width : (section + 2) * width, section * width : (section + 1) * width
        ].set(upper)
        first_pass = first_pass.at[
            : (section + 1) * width, section * width : (section + 1) * width
        ].set(first)
        blocks.append(current)
        full = current
    basis = jnp.concatenate(blocks, axis=1) * jnp.float32(N**0.5)
    return (basis, projection, first_pass)


def solution(mesh):
    return jax.shard_map(
        local,
        mesh=mesh,
        in_specs=(P("row", "col"), P()),
        out_specs=(P("row", None), P(), P()),
        check_vma=False,
    )
```

profile of v0, /device:TPU:0, one launch (start us, length us, event | category | flops | bytes accessed | tf_op | source)
XLA Modules:
  0.0 872.2 jit_solution(4701074359064413226)
XLA Ops:
  7.9 31.2 %copy.5 = f32[4096,2048]{0,1:T(8,128)} copy(f32[4096,2048]{1,0:T(8,128)} %param.17) | data formatting | bytes 67108864 | tf_op args[0]
  39.1 12.8 %gather_fusion = f32[128,4096]{1,0:T(8,128)S(1)} fusion(f32[4096,2048]{0,1:T(8,128)} %copy.5, s32[1024]{0:T(1024)S(1)} %pad_clamp_fusion), kind=kCustom, calls=%fused_computation | custom fusion | bytes 4194816 | tf_op jit(solution)/shard_map/jit(_take)/gather | solution.py:32
  53.6 68.0 %all-reduce.13.cloned.1.call-done = f32[4096,128]{0,1:T(8,128)} async-done(((f32[4096,128]{0,1:T(8,128)}), f32[4096,128]{0,1:T(8,128)}) %all-reduce.13.cloned.1.call-update) | async-done | bytes 2097168 | tf_op jit(solution)/shard_map/psum | solution.py:33
  126.8 41.3 %all-reduce.15.cloned.1.call-done = f32[128,128]{0,1:T(8,128)} async-done(((f32[128,128]{0,1:T(8,128)}), f32[128,128]{0,1:T(8,128)}) %all-reduce.15.cloned.1.call-update) | async-done | bytes 65552 | tf_op jit(solution)/shard_map/psum | solution.py:34
  169.8 11.7 %cholesky.59 = f32[128,128]{1,0:T(8,128)S(1)} custom-call(f32[128,128]{1,0:T(8,128)S(1)} %fusion.15), custom_call_target="Cholesky" | custom-call | tf_op jit(solution)/shard_map/jit(cholesky)/cholesky | solution.py:15
  182.9 9.8 %custom-call.7 = f32[1,128,128]{1,2,0:T(8,128)S(1)} custom-call(f32[1,128,128]{2,1,0:T(8,128)S(1)} %fusion.9), custom_call_target="InvertDiagBlocksLowerTriangular" | custom-call | tf_op jit(solution)/shard_map/jit(_solve_triangular)/triangular_solve | solution.py:16
  196.5 87.1 %all-gather.3.cloned.1.call-done = f32[16384,128]{0,1:T(8,128)} async-done(((f32[4096,128]{0,1:T(8,128)}), f32[16384,128]{0,1:T(8,128)}) %all-gather.3.cloned.1.call-update) | async-done | bytes 8388624 | tf_op jit(solution)/shard_map/all_gather | solution.py:21
  283.6 39.2 %convolution_bitcast_fusion.3 = f32[4096,128]{0,1:T(8,128)} fusion(f32[4096,2048]{1,0:T(8,128)} %param.17, f32[16384,128]{0,1:T(8,128)} %all-gather.3.cloned.1.call-done, s32[]{:T(128)S(6)} %select_n.23), kind=kOutput, calls=%fused_computation.11 | convolution fusion | flops 12884901888 | bytes 36700164 | tf_op jit(solution)/shard_map/dot_general | solution.py:11
  322.9 65.2 %all-reduce.17.cloned.1.call-done = f32[4096,128]{0,1:T(8,128)} async-done(((f32[4096,128]{0,1:T(8,128)}), f32[4096,128]{0,1:T(8,128)}) %all-reduce.17.cloned.1.call-update) | async-done | bytes 2097168 | tf_op jit(solution)/shard_map/psum | solution.py:44
  392.4 41.4 %all-reduce.19.cloned.1.call-done = f32[128,128]{1,0:T(8,128)} async-done(((f32[128,128]{1,0:T(8,128)}), f32[128,128]{1,0:T(8,128)}) %all-reduce.19.cloned.1.call-update) | async-done | bytes 65552 | tf_op jit(solution)/shard_map/psum | solution.py:45
  442.7 42.2 %all-reduce.27.cloned.1.call-done = (f32[128,128]{1,0:T(8,128)}, f32[128,128]{0,1:T(8,128)}) async-done(((f32[128,128]{1,0:T(8,128)}, f32[128,128]{0,1:T(8,128)}), (f32[128,128]{1,0:T(8,128)}, f32[128,128]{0,1:T(8,128)})) %all-reduce.27.cloned.1.call-update) | async-done | bytes 131088 | tf_op jit(solution)/shard_map/psum | solution.py:47
  484.9 5.0 fusion.1
  490.3 11.7 %cholesky.70 = f32[128,128]{1,0:T(8,128)S(1)} custom-call(f32[128,128]{1,0:T(8,128)S(1)} %fusion.13), custom_call_target="Cholesky" | custom-call | tf_op jit(solution)/shard_map/jit(cholesky)/cholesky | solution.py:15
  503.3 9.8 %custom-call.8 = f32[1,128,128]{1,2,0:T(8,128)S(1)} custom-call(f32[1,128,128]{2,1,0:T(8,128)S(1)} %get-tuple-element.91), custom_call_target="InvertDiagBlocksLowerTriangular" | custom-call | tf_op jit(solution)/shard_map/jit(_solve_triangular)/triangular_solve | solution.py:16
  518.5 87.2 %all-gather.5.cloned.1.call-done = f32[16384,128]{0,1:T(8,128)} async-done(((f32[4096,128]{0,1:T(8,128)}), f32[16384,128]{0,1:T(8,128)}) %all-gather.5.cloned.1.call-update) | async-done | bytes 8388624 | tf_op jit(solution)/shard_map/all_gather | solution.py:21
  605.7 39.1 %convolution_bitcast_fusion.1 = f32[4096,128]{0,1:T(8,128)} fusion(f32[4096,2048]{1,0:T(8,128)} %param.17, f32[16384,128]{0,1:T(8,128)} %all-gather.5.cloned.1.call-done, s32[]{:T(128)S(6)} %select_n.23), kind=kOutput, calls=%fused_computation.6 | convolution fusion | flops 12884901888 | bytes 36700164 | tf_op jit(solution)/shard_map/dot_general | solution.py:11
  644.9 65.2 %all-reduce.21.cloned.1.call-done = f32[4096,128]{0,1:T(8,128)} async-done(((f32[4096,128]{0,1:T(8,128)}), f32[4096,128]{0,1:T(8,128)}) %all-reduce.21.cloned.1.call-update) | async-done | bytes 2097168 | tf_op jit(solution)/shard_map/psum | solution.py:44
  710.1 6.3 fusion.5
  717.3 41.1 %all-reduce.23.cloned.1.call-done = f32[256,128]{1,0:T(8,128)} async-done(((f32[256,128]{1,0:T(8,128)}), f32[256,128]{1,0:T(8,128)}) %all-reduce.23.cloned.1.call-update) | async-done | bytes 131088 | tf_op jit(solution)/shard_map/psum | solution.py:45
  770.8 42.0 %all-reduce.25.cloned.1.call-done = (f32[256,128]{1,0:T(8,128)}, f32[128,128]{0,1:T(8,128)}) async-done(((f32[256,128]{1,0:T(8,128)}, f32[128,128]{0,1:T(8,128)}), (f32[256,128]{1,0:T(8,128)}, f32[128,128]{0,1:T(8,128)})) %all-reduce.25.cloned.1.call-update) | async-done | bytes 196624 | tf_op jit(solution)/shard_map/psum | solution.py:47
  812.8 6.1 fusion
  824.5 11.7 %cholesky.81 = f32[128,128]{1,0:T(8,128)S(1)} custom-call(f32[128,128]{1,0:T(8,128)S(1)} %fusion.11), custom_call_target="Cholesky" | custom-call | tf_op jit(solution)/shard_map/jit(cholesky)/cholesky | solution.py:15
  837.7 9.8 %custom-call.9 = f32[1,128,128]{1,2,0:T(8,128)S(1)} custom-call(f32[1,128,128]{2,1,0:T(8,128)S(1)} %get-tuple-element.89), custom_call_target="InvertDiagBlocksLowerTriangular" | custom-call | tf_op jit(solution)/shard_map/jit(_solve_triangular)/triangular_solve | solution.py:16
  854.2 6.6 copy.18
  (93 shorter events, 66.1 us)
Async XLA Ops:
  7.2 114.4 %all-reduce.13.cloned.1.call-start = ((), (), s32[]{:S(2)}) async-start(), calls=%async_computation | async-start | bytes 4194304 | tf_op jit(solution)/shard_map/psum | solution.py:33
  53.5 114.5 %all-reduce.15.cloned.1.call-start = ((), (), s32[]{:S(2)}) async-start(), calls=%async_computation.1 | async-start | bytes 131072 | tf_op jit(solution)/shard_map/psum | solution.py:34
  121.6 71.1 %copy-start.5 = (f32[4096,128]{0,1:T(8,128)S(1)}, f32[4096,128]{0,1:T(8,128)}, u32[]{:S(2)}) copy-start(f32[4096,128]{0,1:T(8,128)} %all-reduce.13.cloned.1.call-done) | copy-start | bytes 6291460
  126.4 157.2 %all-gather.3.cloned.1.call-start = ((), (), s32[]{:S(2)}) async-start(), calls=%async_computation.2 | async-start | bytes 10485760 | tf_op jit(solution)/shard_map/all_gather | solution.py:21
  196.0 192.1 %all-reduce.17.cloned.1.call-start = ((), (), s32[]{:S(2)}) async-start(), calls=%async_computation.3 | async-start | bytes 4194304 | tf_op jit(solution)/shard_map/psum | solution.py:44
  322.8 65.3 %copy-start = (f32[128,4096]{1,0:T(8,128)S(1)}, f32[128,4096]{1,0:T(8,128)}, u32[]{:S(2)}) copy-start(f32[128,4096]{1,0:T(8,128)} %fusion.2) | copy-start | bytes 6291460
  322.9 110.9 %all-reduce.19.cloned.1.call-start = ((), (), s32[]{:S(2)}) async-start(), calls=%async_computation.4 | async-start | bytes 131072 | tf_op jit(solution)/shard_map/psum | solution.py:45
  392.2 92.7 %all-reduce.27.cloned.1.call-start = ((), (), s32[]{:S(2)}) async-start(), calls=%async_computation.9 | async-start | bytes 262144 | tf_op jit(solution)/shard_map/psum | solution.py:47
  437.5 2.5 copy-start.3
  442.5 163.2 %all-gather.5.cloned.1.call-start = ((), (), s32[]{:S(2)}) async-start(), calls=%async_computation.5 | async-start | bytes 10485760 | tf_op jit(solution)/shard_map/all_gather | solution.py:21
  484.9 5.0 copy-start.8
  484.9 5.0 copy-start.13
  518.0 192.1 %all-reduce.21.cloned.1.call-start = ((), (), s32[]{:S(2)}) async-start(), calls=%async_computation.6 | async-start | bytes 4194304 | tf_op jit(solution)/shard_map/psum | solution.py:44
  644.8 113.6 %all-reduce.23.cloned.1.call-start = ((), (), s32[]{:S(2)}) async-start(), calls=%async_computation.7 | async-start | bytes 262144 | tf_op jit(solution)/shard_map/psum | solution.py:45
  716.4 96.3 %all-reduce.25.cloned.1.call-start = ((), (), s32[]{:S(2)}) async-start(), calls=%async_computation.8 | async-start | bytes 393216 | tf_op jit(solution)/shard_map/psum | solution.py:47
  758.4 5.0 copy-start.1
  763.4 4.1 copy-start.4
  767.5 3.1 copy-start.7
  812.8 6.1 copy-start.6
  812.8 6.1 copy-start.10
  812.8 11.2 %copy-start.12 = (f32[128,128]{0,1:T(8,128)S(1)}, f32[128,128]{0,1:T(8,128)}, u32[]{:S(2)}) copy-start(f32[128,128]{0,1:T(8,128)} %get-tuple-element.81) | copy-start | bytes 196612
  847.5 3.7 copy-start.2
  863.6 0.7 copy-start.11
  864.4 0.7 copy-start.9
Sparse Core Ops, SparseCore 0:
  53.6 67.8 all-reduce.12
  126.5 41.4 all-reduce.14
  196.1 87.4 all-gather.2
  323.0 65.0 all-reduce.16
  392.3 41.4 all-reduce.18
  442.6 42.2 all-reduce.26
  518.1 87.4 all-gather.4
  645.0 65.1 all-reduce.20
  716.5 41.8 all-reduce.22
  770.1 42.6 all-reduce.24
where the time goes:
time: 877 us; the launch traced here: 872 us
  waiting for transfers between devices  581 us (66%)
  matrix products  137 us (16%)
  other arithmetic  77.5 us (9%)
  local copies, waits for them, and re-layouts  59.9 us (7%)
  between operations  14.7 us (2%)
    all_gather x2, waiting for transfers between devices, transpose_block(): whole = lax.all_gather(current, 'row', axis=0, tiled=True)  174 us
    psum x2, waiting for transfers between devices, local(): image = lax.psum(partial_value, 'col')  130 us
    dot_general x15, matrix products, product(): jnp.dot(left, right, precision=lax.Precision.HIGHEST, preferred_element_t...  125 us
    psum x2, waiting for transfers between devices, local(): lax.psum((product(stacked.T, once), product(once.T, once)), 'row')  84.2 us
    psum x2, waiting for transfers between devices, local(): first = lax.psum(product(stacked.T, image), 'row')  82.5 us
    psum x1, waiting for transfers between devices, local(): start = lax.psum(jnp.where(inside[None, :], picked, 0.0), 'col')  68 us
    psum x1, waiting for transfers between devices, local(): gram = lax.psum(product(start.T, start), 'row')  41.3 us
    unnamed x30, local copies, waits for them, and re-layouts  39.2 us
  transfers between devices with their start and end apart: 10, of which 10 were waited for; matrix products, arithmetic and copies ran while one was open for 0% of the time, Pallas kernels for 0%

commit v1 on v0

--- a/solution.py
+++ b/solution.py
@@ -41,7 +41,9 @@
         vector = transpose_block(full, col_place, col_count)
         partial_value = product(covariance, vector)
         stacked = jnp.concatenate(blocks, axis=1)
-        image = lax.psum(partial_value, "col")
+        image = partial_value
+        for hop in (1, 2, 4):
+            image = image + lax.ppermute(image, "col", [(dev, dev ^ hop) for dev in range(8)])
         first = lax.psum(product(stacked.T, image), "row")
         once = image - product(stacked, first)
         second, raw_gram = lax.psum((product(stacked.T, once), product(once.T, once)), "row")

time: 877 us -> 1040 us (1.19)
  waiting for transfers between devices: 581 us -> 731 us
    ppermute x0 -> x6, waiting for transfers between devices: none -> 280 us  [local(): lax.ppermute(image, 'col', [(dev, dev ^ hop) for dev in range(8)])]
    psum x2 -> x0, waiting for transfers between devices: 130 us -> none  [local(): image = lax.psum(partial_value, 'col')]
    unnamed x30 -> x38, local copies, waits for them, and re-layouts: 39.2 us -> 43.1 us
  transfers between devices with their start and end apart: 10 -> 14, of which waited for: 10 -> 14; matrix products, arithmetic and copies ran while one was open for 0% -> 0% of each run, Pallas kernels for 0% -> 0%
where the time goes in v1:
time: 1040 us; the launch traced here: 1030 us
  waiting for transfers between devices  731 us (70%)
  matrix products  133 us (13%)
  other arithmetic  82.3 us (8%)
  local copies, waits for them, and re-layouts  63.8 us (6%)
  between operations  14.8 us (1%)
    ppermute x6, waiting for transfers between devices, local(): lax.ppermute(image, 'col', [(dev, dev ^ hop) for dev in range(8)])  280 us
    all_gather x2, waiting for transfers between devices, transpose_block(): whole = lax.all_gather(current, 'row', axis=0, tiled=True)  174 us
    dot_general x15, matrix products, product(): jnp.dot(left, right, precision=lax.Precision.HIGHEST, preferred_element_t...  121 us
    psum x2, waiting for transfers between devices, local(): lax.psum((product(stacked.T, once), product(once.T, once)), 'row')  84.2 us
    psum x2, waiting for transfers between devices, local(): first = lax.psum(product(stacked.T, image), 'row')  83.2 us
    psum x1, waiting for transfers between devices, local(): start = lax.psum(jnp.where(inside[None, :], picked, 0.0), 'col')  68 us
    unnamed x38, local copies, waits for them, and re-layouts  43.1 us
    psum x1, waiting for transfers between devices, local(): gram = lax.psum(product(start.T, start), 'row')  41.3 us
  transfers between devices with their start and end apart: 14, of which 14 were waited for; matrix products, arithmetic and copies ran while one was open for 0% of the time, Pallas kernels for 0%

profile of v1, /device:TPU:0, one launch (start us, length us, event | category | flops | bytes accessed | tf_op | source)
XLA Modules:
  0.0 1034.8 jit_solution(2351387053976268932)
XLA Ops:
  7.9 31.1 %copy.5 = f32[4096,2048]{0,1:T(8,128)} copy(f32[4096,2048]{1,0:T(8,128)} %param.17) | data formatting | bytes 67108864 | tf_op args[0]
  39.0 12.8 %gather_fusion = f32[128,4096]{1,0:T(8,128)S(1)} fusion(f32[4096,2048]{0,1:T(8,128)} %copy.5, s32[1024]{0:T(1024)S(1)} %pad_clamp_fusion), kind=kCustom, calls=%fused_computation | custom fusion | bytes 4194816 | tf_op jit(solution)/shard_map/jit(_take)/gather | solution.py:32
  53.5 68.0 %all-reduce.11.cloned.1.call-done = f32[4096,128]{0,1:T(8,128)} async-done(((f32[4096,128]{0,1:T(8,128)}), f32[4096,128]{0,1:T(8,128)}) %all-reduce.11.cloned.1.call-update) | async-done | bytes 2097168 | tf_op jit(solution)/shard_map/psum | solution.py:33
  126.7 41.3 %all-reduce.13.cloned.1.call-done = f32[128,128]{0,1:T(8,128)} async-done(((f32[128,128]{0,1:T(8,128)}), f32[128,128]{0,1:T(8,128)}) %all-reduce.13.cloned.1.call-update) | async-done | bytes 65552 | tf_op jit(solution)/shard_map/psum | solution.py:34
  169.8 11.7 %cholesky.59 = f32[128,128]{1,0:T(8,128)S(1)} custom-call(f32[128,128]{1,0:T(8,128)S(1)} %fusion.15), custom_call_target="Cholesky" | custom-call | tf_op jit(solution)/shard_map/jit(cholesky)/cholesky | solution.py:15
  182.8 9.8 custom-call.7
  196.5 87.1 %all-gather.3.cloned.1.call-done = f32[16384,128]{0,1:T(8,128)} async-done(((f32[4096,128]{0,1:T(8,128)}), f32[16384,128]{0,1:T(8,128)}) %all-gather.3.cloned.1.call-update) | async-done | bytes 8388624 | tf_op jit(solution)/shard_map/all_gather | solution.py:21
  283.6 38.4 %convolution_bitcast_fusion.3 = f32[4096,128]{0,1:T(8,128)S(1)} fusion(f32[4096,2048]{1,0:T(8,128)} %param.17, f32[16384,128]{0,1:T(8,128)} %all-gather.3.cloned.1.call-done, s32[]{:T(128)S(6)} %select_n.23), kind=kOutput, calls=%fused_computation.11 | convolution fusion | flops 12884901888 | bytes 36700164 | tf_op jit(solution)/shard_map/dot_general | solution.py:11
  329.6 46.2 %collective-permute-done.1 = f32[4096,128]{0,1:T(8,128)S(1)} collective-permute-done((f32[4096,128]{0,1:T(8,128)S(1)}, f32[4096,128]{0,1:T(8,128)S(1)}, u32[]{:S(2)}, u32[]{:S(2)}) %collective-permute-start.1) | collective-permute-done | bytes 2097184 | tf_op jit(solution)/shard_map/ppermute | solution.py:46
  378.5 90.3 %collective-permute-done.2 = f32[4096,128]{0,1:T(8,128)S(1)} collective-permute-done((f32[4096,128]{0,1:T(8,128)S(1)}, f32[4096,128]{0,1:T(8,128)S(1)}, u32[]{:S(2)}, u32[]{:S(2)}) %collective-permute-start.2) | collective-permute-done | bytes 2097184 | tf_op jit(solution)/shard_map/ppermute | solution.py:46
  473.1 41.7 %all-reduce.15.cloned.1.call-done = f32[128,128]{1,0:T(8,128)} async-done(((f32[128,128]{1,0:T(8,128)}), f32[128,128]{1,0:T(8,128)}) %all-reduce.15.cloned.1.call-update) | async-done | bytes 65552 | tf_op jit(solution)/shard_map/psum | solution.py:47
  523.8 42.2 %all-reduce.21.cloned.1.call-done = (f32[128,128]{1,0:T(8,128)}, f32[128,128]{0,1:T(8,128)}) async-done(((f32[128,128]{1,0:T(8,128)}, f32[128,128]{0,1:T(8,128)}), (f32[128,128]{1,0:T(8,128)}, f32[128,128]{0,1:T(8,128)})) %all-reduce.21.cloned.1.call-update) | async-done | bytes 131088 | tf_op jit(solution)/shard_map/psum | solution.py:49
  571.3 11.7 %cholesky.70 = f32[128,128]{1,0:T(8,128)S(1)} custom-call(f32[128,128]{1,0:T(8,128)S(1)} %fusion.13), custom_call_target="Cholesky" | custom-call | tf_op jit(solution)/shard_map/jit(cholesky)/cholesky | solution.py:15
  584.4 9.8 custom-call.8
  599.6 87.2 %all-gather.5.cloned.1.call-done = f32[16384,128]{0,1:T(8,128)} async-done(((f32[4096,128]{0,1:T(8,128)}), f32[16384,128]{0,1:T(8,128)}) %all-gather.5.cloned.1.call-update) | async-done | bytes 8388624 | tf_op jit(solution)/shard_map/all_gather | solution.py:21
  686.8 39.1 %convolution_bitcast_fusion.1 = f32[4096,128]{0,1:T(8,128)} fusion(f32[4096,2048]{1,0:T(8,128)} %param.17, f32[16384,128]{0,1:T(8,128)} %all-gather.5.cloned.1.call-done, s32[]{:T(128)S(6)} %select_n.23), kind=kOutput, calls=%fused_computation.6 | convolution fusion | flops 12884901888 | bytes 36700164 | tf_op jit(solution)/shard_map/dot_general | solution.py:11
  733.7 46.2 %collective-permute-done.4 = f32[4096,128]{0,1:T(8,128)S(1)} collective-permute-done((f32[4096,128]{0,1:T(8,128)S(1)}, f32[4096,128]{0,1:T(8,128)S(1)}, u32[]{:S(2)}, u32[]{:S(2)}) %collective-permute-start.4) | collective-permute-done | bytes 2097184 | tf_op jit(solution)/shard_map/ppermute | solution.py:46
  782.6 90.2 %collective-permute-done.5 = f32[4096,128]{0,1:T(8,128)S(1)} collective-permute-done((f32[4096,128]{0,1:T(8,128)S(1)}, f32[4096,128]{0,1:T(8,128)S(1)}, u32[]{:S(2)}, u32[]{:S(2)}) %collective-permute-start.5) | collective-permute-done | bytes 2097184 | tf_op jit(solution)/shard_map/ppermute | solution.py:46
  879.5 41.5 %all-reduce.17.cloned.1.call-done = f32[256,128]{1,0:T(8,128)} async-done(((f32[256,128]{1,0:T(8,128)}), f32[256,128]{1,0:T(8,128)}) %all-reduce.17.cloned.1.call-update) | async-done | bytes 131088 | tf_op jit(solution)/shard_map/psum | solution.py:47
  933.3 42.0 %all-reduce.19.cloned.1.call-done = (f32[256,128]{1,0:T(8,128)}, f32[128,128]{0,1:T(8,128)}) async-done(((f32[256,128]{1,0:T(8,128)}, f32[128,128]{0,1:T(8,128)}), (f32[256,128]{1,0:T(8,128)}, f32[128,128]{0,1:T(8,128)})) %all-reduce.19.cloned.1.call-update) | async-done | bytes 196624 | tf_op jit(solution)/shard_map/psum | solution.py:49
  975.3 6.1 fusion
  987.1 11.7 %cholesky.81 = f32[128,128]{1,0:T(8,128)S(1)} custom-call(f32[128,128]{1,0:T(8,128)S(1)} %fusion.11), custom_call_target="Cholesky" | custom-call | tf_op jit(solution)/shard_map/jit(cholesky)/cholesky | solution.py:15
  1000.2 9.8 custom-call.9
  1016.8 6.6 copy.18
  (113 shorter events, 97.6 us)
Async XLA Ops:
  7.2 114.4 %all-reduce.11.cloned.1.call-start = ((), (), s32[]{:S(2)}) async-start(), calls=%async_computation | async-start | bytes 4194304 | tf_op jit(solution)/shard_map/psum | solution.py:33
  53.5 114.5 %all-reduce.13.cloned.1.call-start = ((), (), s32[]{:S(2)}) async-start(), calls=%async_computation.1 | async-start | bytes 131072 | tf_op jit(solution)/shard_map/psum | solution.py:34
  121.5 71.1 %copy-start.8 = (f32[4096,128]{0,1:T(8,128)S(1)}, f32[4096,128]{0,1:T(8,128)}, u32[]{:S(2)}) copy-start(f32[4096,128]{0,1:T(8,128)} %all-reduce.11.cloned.1.call-done) | copy-start | bytes 6291460
  126.4 157.2 %all-gather.3.cloned.1.call-start = ((), (), s32[]{:S(2)}) async-start(), calls=%async_computation.2 | async-start | bytes 10485760 | tf_op jit(solution)/shard_map/all_gather | solution.py:21
  195.9 318.9 %all-reduce.15.cloned.1.call-start = ((), (), s32[]{:S(2)}) async-start(), calls=%async_computation.3 | async-start | bytes 131072 | tf_op jit(solution)/shard_map/psum | solution.py:47
  322.0 4.2 collective-permute-start
  328.0 47.7 %collective-permute-start.1 = (f32[4096,128]{0,1:T(8,128)S(1)}, f32[4096,128]{0,1:T(8,128)S(1)}, u32[]{:S(2)}, u32[]{:S(2)}) collective-permute-start(f32[4096,128]{0,1:T(8,128)S(1)} %add.77), channel_id=1, source_target_pairs={{0,2},{1,3},{2,0},{3,1},{4,6},{5,7},{6,4},{7,5},{8,10},{9,11},{10,... | collective-permute-start | bytes 6291464 | tf_op jit(solution)/shard_map/ppermute | solution.py:46
  376.1 94.3 %copy-start = (f32[128,4096]{1,0:T(8,128)S(1)}, f32[128,4096]{1,0:T(8,128)}, u32[]{:S(2)}) copy-start(f32[128,4096]{1,0:T(8,128)} %fusion.2) | copy-start | bytes 6291460
  376.1 92.7 %collective-permute-start.2 = (f32[4096,128]{0,1:T(8,128)S(1)}, f32[4096,128]{0,1:T(8,128)S(1)}, u32[]{:S(2)}, u32[]{:S(2)}) collective-permute-start(f32[4096,128]{0,1:T(8,128)S(1)} %add.78), channel_id=1, source_target_pairs={{0,4},{1,5},{2,6},{3,7},{4,0},{5,1},{6,2},{7,3},{8,12},{9,13},{10,... | collective-permute-start | bytes 6291464 | tf_op jit(solution)/shard_map/ppermute | solution.py:46
  472.9 93.0 %all-reduce.21.cloned.1.call-start = ((), (), s32[]{:S(2)}) async-start(), calls=%async_computation.7 | async-start | bytes 262144 | tf_op jit(solution)/shard_map/psum | solution.py:49
  523.5 163.2 %all-gather.5.cloned.1.call-start = ((), (), s32[]{:S(2)}) async-start(), calls=%async_computation.4 | async-start | bytes 10485760 | tf_op jit(solution)/shard_map/all_gather | solution.py:21
  565.9 5.0 copy-start.12
  566.0 5.0 copy-start.17
  599.1 321.8 %all-reduce.17.cloned.1.call-start = ((), (), s32[]{:S(2)}) async-start(), calls=%async_computation.5 | async-start | bytes 262144 | tf_op jit(solution)/shard_map/psum | solution.py:47
  725.9 4.4 collective-permute-start.3
  732.1 47.7 %collective-permute-start.4 = (f32[4096,128]{0,1:T(8,128)S(1)}, f32[4096,128]{0,1:T(8,128)S(1)}, u32[]{:S(2)}, u32[]{:S(2)}) collective-permute-start(f32[4096,128]{0,1:T(8,128)S(1)} %add.80), channel_id=1, source_target_pairs={{0,2},{1,3},{2,0},{3,1},{4,6},{5,7},{6,4},{7,5},{8,10},{9,11},{10,... | collective-permute-start | bytes 6291464 | tf_op jit(solution)/shard_map/ppermute | solution.py:46
  780.1 94.4 %copy-start.1 = (f32[4096,128]{0,1:T(8,128)S(1)}, f32[4096,128]{0,1:T(8,128)}, u32[]{:S(2)}) copy-start(f32[4096,128]{0,1:T(8,128)} %convolution_bitcast_fusion.2) | copy-start | bytes 6291460
  780.1 92.7 %collective-permute-start.5 = (f32[4096,128]{0,1:T(8,128)S(1)}, f32[4096,128]{0,1:T(8,128)S(1)}, u32[]{:S(2)}, u32[]{:S(2)}) collective-permute-start(f32[4096,128]{0,1:T(8,128)S(1)} %add.81), channel_id=1, source_target_pairs={{0,4},{1,5},{2,6},{3,7},{4,0},{5,1},{6,2},{7,3},{8,12},{9,13},{10,... | collective-permute-start | bytes 6291464 | tf_op jit(solution)/shard_map/ppermute | solution.py:46
  878.6 96.7 %all-reduce.19.cloned.1.call-start = ((), (), s32[]{:S(2)}) async-start(), calls=%async_computation.6 | async-start | bytes 393216 | tf_op jit(solution)/shard_map/psum | solution.py:49
  921.0 5.0 copy-start.2
  926.0 4.1 copy-start.5
  975.3 6.1 copy-start.10
  975.3 6.1 copy-start.14
  975.3 11.2 %copy-start.16 = (f32[128,128]{0,1:T(8,128)S(1)}, f32[128,128]{0,1:T(8,128)}, u32[]{:S(2)}) copy-start(f32[128,128]{0,1:T(8,128)} %get-tuple-element.81) | copy-start | bytes 196612
  (8 other events, 14.7 us)
Sparse Core Ops, SparseCore 0:
  53.6 67.8 all-reduce.10
  126.5 41.4 all-reduce.12
  196.0 87.4 all-gather.2
  473.0 41.7 all-reduce.14
  523.6 42.2 all-reduce.20
  599.2 87.4 all-gather.4
  878.7 42.1 all-reduce.16
  932.6 42.6 all-reduce.18
